TPU v7x, 256 devices: a whole 4x4x8 slice. The times are simulated.
256 devices in a mesh: gx: 32 (over z, x_hi, core), gy: 8 (over x_lo, y).
Axes of the slice: x: 4 (x_hi: 2, x_lo: 2; x = x_hi * 2 + x_lo), y: 4, z: 8, core: 2. Of those that a mesh axis runs over, the one named last changes fastest.
Arguments:
- positions: float32 [3, 12, 64, 128, 256], P(None, None, 'gx', 'gy'), may hold values from 0 to 1
- velocities: float32 [3, 12, 64, 128, 256], P(None, None, 'gx', 'gy'), may hold values from -6 to 6
- thermal: float32 [3, 12, 64, 128, 256], P(None, None, 'gx', 'gy'), may hold values from -6 to 6
- offsets: int32 [12, 64, 128, 256], P(None, 'gx', 'gy'), may hold values from 0 to 7
- occupancy: int32 [12, 64, 128, 256], P(None, 'gx', 'gy'), may hold values from 0 to 1, as said below
- shift_codes: int32 [3], replicated, may hold values from 0 to 7
Outputs:
- new_velocities: float32 [3, 12, 64, 128, 256], P(None, None, 'gx', 'gy')
Inputs may be any that keep to these rules, and one draw needn't show every extreme that they name: `occupancy`: the particles of a storage cell occupy its first slots; every storage cell holds 8 to 12 particles.
All inputs are finite; a program needn't handle non-finite values.
Results may differ from a plain program's by a relative error of at most 0.0001.
Values sent between devices are 32-bit elements; how exact they have to be, the bound alone decides.
A program may use at most 64 MiB of HBM per device.

v0:
```python
import functools

import jax
import jax.numpy as jnp
from jax import lax
from jax.experimental import pallas as pl
from jax.experimental.pallas import tpu as pltpu
from jax.sharding import PartitionSpec as P

MESH = pl.DeviceIdType.MESH
f32 = jnp.float32
SLOTS = 12
ridge = 0.5

O, M, I = 0, 1, 2
ROW_PARTS = {O: ((0, 1),), M: ((0, 0), (1, 0)), I: ((1, 1),)}
STATIC, DYNAMIC = 10, 6
FIELDS = (STATIC, DYNAMIC) * 3
XMSG = ("bulk", "edge", "dup", "ddown")


def kernel(
    shift_ref, pos_h, vel_h, th_h, off_h, occ_h, out_ref,
    pos, vel, th, off, occ, code, gs, gd, wb,
    es0, ed0, es1, ed1, es2, ed2,
    rb0, rb1, rb2, rb3, rb4, rb5,
    sd, su, sdz, ru, rd, rxe, rxu, rxd, cm, ct, op, ope, tm, te, tr,
    in_sem, out_sem, s_sem, r_sem,
):
    es, ed = (es0, es1, es2), (ed0, ed1, ed2)
    e = (es0, ed0, es1, ed1, es2, ed2)
    rb = (rb0, rb1, rb2, rb3, rb4, rb5)
    gx, gy = lax.axis_index("gx"), lax.axis_index("gy")
    ngx, ngy = lax.axis_size("gx"), lax.axis_size("gy")
    core = lax.rem(gx, 2)
    off_gx = lax.rem(gx + 2 * core - 1 + ngx, ngx)
    on_gx = gx + 1 - 2 * core
    up, down = lax.rem(gy + 1, ngy), lax.rem(gy + ngy - 1, ngy)
    rows = (core, 1 - core)
    sh = [shift_ref[0], shift_ref[1], shift_ref[2]]

    copies = []
    for r in (0, 1):
        for t, (src, dst) in enumerate(((off_h, off), (occ_h, occ), (pos_h, pos), (th_h, th), (vel_h, vel))):
            view = src.at[:, rows[r]] if t < 2 else src.at[:, :, rows[r]]
            c = pltpu.make_async_copy(view, dst.at[r], in_sem.at[r, t])
            c.start()
            copies.append(c)

    barrier = pltpu.get_barrier_semaphore()
    for to in ((off_gx, gy), (on_gx, gy), (gx, up), (gx, down), (off_gx, up), (off_gx, down), (on_gx, up), (on_gx, down)):
        pl.semaphore_signal(barrier, inc=1, device_id=to, device_id_type=MESH)

    core_f = core.astype(f32)
    xbit = {(0, 1): 1.0 - core_f, (0, 0): core_f, (1, 1): core_f, (1, 0): 1.0 - core_f}
    flip = (core * 4, (1 - core) * 4)

    def chunked(body):
        def step(t, carry):
            ys = pl.ds(pl.multiple_of(8 * (t // 2), 8), 8)
            zs = pl.ds(pl.multiple_of(128 * lax.rem(t, 2), 128), 128)
            body(ys, zs)
            return carry
        lax.fori_loop(0, 4, step, 0)

    def make_codes(r):
        x = sh[0] ^ flip[r]
        for m in range(SLOTS):
            code[r, m] = jnp.where(occ[r, m] == 1, off[r, m] ^ x, 8)

    def accumulate(acc, mask, vals):
        for f, v in enumerate(vals):
            term = jnp.where(mask, v, 0.0)
            acc[f] = term if acc[f] is None else acc[f] + term

    def static_moments(r, p):
        def body(ys, zs):
            acc = [[None] * STATIC for _ in range(4)]
            for m in range(SLOTS):
                k = code[r, m, ys, zs]
                x, y, z = (pos[r, a, m, ys, zs] for a in range(3))
                vals = [1.0, x, y, z, x * x, y * y, z * z, x * y, x * z, y * z]
                for q in range(4):
                    accumulate(acc[q], k == p * 4 + q, vals)
            for q in range(4):
                for f in range(STATIC):
                    gs[r, p * 4 + q, f, ys, zs] = acc[q][f]
        chunked(body)

    def dynamic_moments(s, r, p):
        def body(ys, zs):
            acc = [[None] * DYNAMIC for _ in range(4)]
            for m in range(SLOTS):
                k = code[r, m, ys, zs]
                x, y, z = (pos[r, a, m, ys, zs] for a in range(3))
                if s == 0:
                    w = [vel[r, a, m, ys, zs] - th[r, a, m, ys, zs] for a in range(3)]
                else:
                    w = [th[r, a, (m + s - 1) % SLOTS, ys, zs] - th[r, a, (m + s) % SLOTS, ys, zs] for a in range(3)]
                vals = w + [y * w[2] - z * w[1], z * w[0] - x * w[2], x * w[1] - y * w[0]]
                for q in range(4):
                    accumulate(acc[q], k == p * 4 + q, vals)
            for q in range(4):
                for f in range(DYNAMIC):
                    gd[s, r, p * 4 + q, f, ys, zs] = acc[q][f]
        chunked(body)

    def static_field(load, f, bx, by, bz):
        v = load(f)
        if f == 1:
            v = v + bx * load(0)
        elif f == 2 and by:
            v = v + load(0)
        elif f == 3 and bz:
            v = v + load(0)
        elif f == 4:
            v = v + bx * (2.0 * load(1) + load(0))
        elif f == 5 and by:
            v = v + (2.0 * load(2) + load(0))
        elif f == 6 and bz:
            v = v + (2.0 * load(3) + load(0))
        elif f == 7:
            v = v + bx * (load(2) + load(0) if by else load(2))
            v = v + load(1) if by else v
        elif f == 8:
            v = v + bx * (load(3) + load(0) if bz else load(3))
            v = v + load(1) if bz else v
        elif f == 9:
            if by:
                v = v + load(3)
            if bz:
                v = v + load(2)
            if by and bz:
                v = v + load(0)
        return v

    def dynamic_field(load, f, bx, by, bz):
        v = load(f)
        if f == 3:
            v = v + load(2) if by else v
            v = v - load(1) if bz else v
        elif f == 4:
            v = v - bx * load(2)
            v = v + load(0) if bz else v
        elif f == 5:
            v = v + bx * load(1)
            v = v - load(0) if by else v
        return v

    not_last = lax.broadcasted_iota(jnp.int32, (16, 256), 0) < 15
    is_last = lax.broadcasted_iota(jnp.int32, (16, 256), 0) == 15
    is_first = lax.broadcasted_iota(jnp.int32, (16, 256), 0) == 0

    def assemble(ph, row, source, field):
        n = FIELDS[ph]
        for f in range(n):
            planes = []
            for bz in (0, 1):
                total = [None, None]
                for by in (0, 1):
                    for r, p in ROW_PARTS[row]:
                        load = functools.partial(source, r, p * 4 + by * 2 + bz)
                        v = field(load, f, xbit[r, p], by, bz)
                        total[by] = v if total[by] is None else total[by] + v
                sdz[bz, f : f + 1] = total[1][0:1]
                planes.append(total[0] + jnp.where(not_last, pltpu.roll(total[1], 15, 0), 0.0))
            whole = planes[0] + pltpu.roll(planes[1], 255, 1)
            e[ph][row, f] = whole
            su[ph, row, f : f + 1] = whole[15:16]
        sd[ph, row] = sdz[0] + pltpu.roll(sdz[1], 255, 1)

    def remote(ph, j, src, dst, to):
        return pltpu.make_async_remote_copy(
            src_ref=src, dst_ref=dst, send_sem=s_sem.at[ph, j], recv_sem=r_sem.at[ph, j], device_id=to, device_id_type=MESH
        )

    def messages(ph, row):
        n = 16 if ph == -1 else FIELDS[ph]
        fs = pl.ds(0, 8 if n <= 8 else 16)
        low, high = sd.at[ph, row, fs], su.at[ph, row, fs]
        out = [
            remote(ph, 8 + 2 * row, low, ru.at[ph, row, fs], (gx, down)),
            remote(ph, 9 + 2 * row, high, rd.at[ph, row, fs], (gx, up)),
        ]
        if row != M:
            side = 0 if row == O else 1
            to = off_gx if row == O else on_gx
            out += [
                remote(ph, 4 * side + 2, low, rxu.at[ph, side, fs], (to, down)),
                remote(ph, 4 * side + 3, high, rxd.at[ph, side, fs], (to, up)),
                remote(ph, 4 * side + 1, low, rxe.at[ph, side, fs], (to, gy)),
                remote(ph, 4 * side, e[ph].at[row], rb[ph].at[side], (to, gy)),
            ]
        return out

    def send(ph, row):
        for c in messages(ph, row):
            c.start()

    def receive(ph, row):
        for c in messages(ph, row):
            c.wait_recv()

    def totals(ph, row):
        low, high = sd[ph, row] + rd[ph, row], ru[ph, row]
        if row != M:
            side = 0 if row == O else 1
            low = low + rxe[ph, side] + rxd[ph, side]
            high = high + rxu[ph, side]
        cm[ph, row] = low
        ct[ph, row] = high

    def total(ph, row, f):
        v = e[ph][row, f]
        if row != M:
            v = v + rb[ph][0 if row == O else 1, f]
        return v + jnp.where(is_last, ct[ph, row, f : f + 1], 0.0)

    def invert(a):
        n, sx, sy, sz, xx, yy, zz, xy, xz, yz = a
        inv = 1.0 / jnp.maximum(n, 1.0)
        cx, cy, cz = sx * inv, sy * inv, sz * inv
        mxx, myy, mzz = xx - sx * cx, yy - sy * cy, zz - sz * cz
        kxy, kxz, kyz = sx * cy - xy, sx * cz - xz, sy * cz - yz
        kxx, kyy, kzz = myy + mzz + ridge, mxx + mzz + ridge, mxx + myy + ridge
        axx = kyy * kzz - kyz * kyz
        ayy = kxx * kzz - kxz * kxz
        azz = kxx * kyy - kxy * kxy
        axy = kxz * kyz - kxy * kzz
        axz = kxy * kyz - kxz * kyy
        ayz = kxy * kxz - kxx * kyz
        idet = 1.0 / (kxx * axx + kxy * axy + kxz * axz)
        return [inv, cx, cy, cz, axx * idet, ayy * idet, azz * idet, axy * idet, axz * idet, ayz * idet]

    def respond(o, d):
        inv, cx, cy, cz, axx, ayy, azz, axy, axz, ayz = o
        wx, wy, wz, lx, ly, lz = d
        tx, ty, tz = lx - (cy * wz - cz * wy), ly - (cz * wx - cx * wz), lz - (cx * wy - cy * wx)
        ox = axx * tx + axy * ty + axz * tz
        oy = axy * tx + ayy * ty + ayz * tz
        oz = axz * tx + ayz * ty + azz * tz
        return [wx * inv - (oy * cz - oz * cy), wy * inv - (oz * cx - ox * cz), wz * inv - (ox * cy - oy * cx), ox, oy, oz]

    def static_solve(s, row):
        for f, v in enumerate(invert([total(2 * s, row, f) for f in range(STATIC)])):
            op[row, f] = v
        o = invert([cm[2 * s, row, f : f + 1] for f in range(STATIC)])
        for f, v in enumerate(o):
            ope[row, f : f + 1] = v

    def dynamic_solve(s, row):
        ph = 2 * s + 1
        t = respond([op[row, f] for f in range(STATIC)], [total(ph, row, f) for f in range(DYNAMIC)])
        x = respond([ope[row, f : f + 1] for f in range(STATIC)], [cm[ph, row, f : f + 1] for f in range(DYNAMIC)])
        for f in range(DYNAMIC):
            te[row, f : f + 1] = x[f]
            tm[row, f] = t[f]
        te[row, 8:16] = pltpu.roll(te[row, 0:8], 1, 1)
        for f in range(DYNAMIC):
            v = tm[row, f]
            for bz in (0, 1):
                v = v if bz == 0 else pltpu.roll(v, 1, 1)
                tr[row, bz, f] = v
                tr[row, 2 + bz, f] = jnp.where(is_first, te[row, 8 * bz + f : 8 * bz + f + 1], pltpu.roll(v, 1, 0))

    def offset(t, bx, by, bz):
        ax, ay, az, ox, oy, oz = t
        if bz:
            ax, ay = ax + oy, ay - ox
        if by:
            ax, az = ax - oz, az + ox
        return [ax, ay + bx * oz, az - bx * oy, ox, oy, oz]

    def advance(s, r):
        delta = sh[0] ^ sh[s - 1]
        for p in (0, 1):
            row = M if p == 0 else (O if r == 0 else I)
            for q in range(4):
                g = p * 4 + q
                src = g if s == 1 else g ^ delta
                for h in (0, 1):
                    ys = pl.ds(8 * h, 8)
                    t = [tr[row, q, f, ys] for f in range(6)]
                    ax, ay, az, ox, oy, oz = offset(t, xbit[r, p], q // 2, q % 2)
                    n, x, y, z, xx, yy, zz, xy, xz, yz = (gs[r, src, f, ys] for f in range(STATIC))
                    d = [gd[s, r, src, f, ys] for f in range(6)]
                    wb[s - 1, r, g, 0, ys] = d[0] + n * ax + (oy * z - oz * y)
                    wb[s - 1, r, g, 1, ys] = d[1] + n * ay + (oz * x - ox * z)
                    wb[s - 1, r, g, 2, ys] = d[2] + n * az + (ox * y - oy * x)
                    wb[s - 1, r, g, 3, ys] = d[3] + (y * az - z * ay) + ((yy + zz) * ox - xy * oy - xz * oz)
                    wb[s - 1, r, g, 4, ys] = d[4] + (z * ax - x * az) + ((xx + zz) * oy - xy * ox - yz * oz)
                    wb[s - 1, r, g, 5, ys] = d[5] + (x * ay - y * ax) + ((xx + yy) * oz - xz * ox - yz * oy)

    def static_source(s):
        delta = sh[0] ^ sh[s]
        return lambda r, g, f: gs[r, g if s == 0 else g ^ delta, f]

    def dynamic_source(s):
        if s == 0:
            return lambda r, g, f: gd[0, r, g, f]
        delta = sh[s - 1] ^ sh[s]
        return lambda r, g, f: wb[s - 1, r, g ^ delta, f]

    def finish(r):
        delta = sh[0] ^ sh[2]
        def body(ys, zs):
            tables = []
            for p in (0, 1):
                row = M if p == 0 else (O if r == 0 else I)
                for q in range(4):
                    t = [tr[row, q, f, ys, zs] for f in range(6)]
                    tables.append(offset(t, xbit[r, p], q // 2, q % 2))
            for m in range(SLOTS):
                k = code[r, m, ys, zs] ^ delta
                bz, by, bx = (k & 1) == 1, (k & 2) == 2, (k & 4) == 4
                t = []
                for f in range(6):
                    c = [jnp.where(bz, tables[2 * j + 1][f], tables[2 * j][f]) for j in range(4)]
                    c = [jnp.where(by, c[1], c[0]), jnp.where(by, c[3], c[2])]
                    t.append(jnp.where(bx, c[1], c[0]))
                ax, ay, az, ox, oy, oz = t
                x, y, z = (pos[r, a, m, ys, zs] for a in range(3))
                hot = [th[r, a, (m + 2) % SLOTS, ys, zs] for a in range(3)]
                live = k < 8
                out_ref[0, m, rows[r], ys, zs] = jnp.where(live, hot[0] + ax + (oy * z - oz * y), 0.0)
                out_ref[1, m, rows[r], ys, zs] = jnp.where(live, hot[1] + ay + (oz * x - ox * z), 0.0)
                out_ref[2, m, rows[r], ys, zs] = jnp.where(live, hot[2] + az + (ox * y - oy * x), 0.0)
        chunked(body)

    sdz[...] = jnp.zeros_like(sdz)
    su[...] = jnp.zeros_like(su)
    te[...] = jnp.zeros_like(te)
    for t in range(5):
        copies[t].wait()
    make_codes(0)
    static_moments(0, 1)
    dynamic_moments(0, 0, 1)
    assemble(0, O, static_source(0), static_field)
    assemble(1, O, dynamic_source(0), dynamic_field)
    pl.semaphore_wait(barrier, 8)
    send(0, O)
    send(1, O)
    static_moments(0, 0)
    assemble(2, O, static_source(1), static_field)
    send(2, O)
    dynamic_moments(0, 0, 0)
    for t in range(5, 10):
        copies[t].wait()
    make_codes(1)
    for p in (0, 1):
        static_moments(1, p)
        dynamic_moments(0, 1, p)
    for row in (M, I):
        assemble(0, row, static_source(0), static_field)
        assemble(1, row, dynamic_source(0), dynamic_field)
        send(0, row)
        send(1, row)
    for row in (M, I):
        assemble(2, row, static_source(1), static_field)
        send(2, row)
    for row in (M, I, O):
        assemble(4, row, static_source(2), static_field)
        if row != O:
            send(4, row)
    for r in (0, 1):
        for p in (0, 1):
            dynamic_moments(1, r, p)
    for s in (0, 1, 2):
        for row in (M, I, O):
            receive(2 * s, row)
            totals(2 * s, row)
            static_solve(s, row)
        for row in (M, I, O):
            receive(2 * s + 1, row)
            totals(2 * s + 1, row)
            dynamic_solve(s, row)
        if s < 2:
            advance(s + 1, 0)
            assemble(2 * s + 3, O, dynamic_source(s + 1), dynamic_field)
            send(2 * s + 3, O)
            if s == 0:
                send(4, O)
            advance(s + 1, 1)
            for row in (M, I):
                assemble(2 * s + 3, row, dynamic_source(s + 1), dynamic_field)
                send(2 * s + 3, row)
            if s == 0:
                for r in (0, 1):
                    for p in (0, 1):
                        dynamic_moments(2, r, p)
    for r in (0, 1):
        finish(r)
    for ph in range(6):
        for row in (O, M, I):
            for c in messages(ph, row):
                c.wait_send()


def local(positions, velocities, thermal, offsets, occupancy, shift_codes):
    any_space = pl.BlockSpec(memory_space=pl.ANY)
    rows = lambda n: pltpu.VMEM((n, 16, 256), f32)
    per = lambda *lead: pltpu.VMEM((*lead, 16, 256), f32)
    return pl.pallas_call(
        kernel,
        out_shape=jax.ShapeDtypeStruct(positions.shape, f32),
        in_specs=[pl.BlockSpec(memory_space=pltpu.SMEM)] + [any_space] * 5,
        out_specs=pl.BlockSpec(memory_space=pltpu.VMEM),
        scratch_shapes=[
            per(2, 3, SLOTS), per(2, 3, SLOTS), per(2, 3, SLOTS),
            pltpu.VMEM((2, SLOTS, 16, 256), jnp.int32), pltpu.VMEM((2, SLOTS, 16, 256), jnp.int32), pltpu.VMEM((2, SLOTS, 16, 256), jnp.int32),
            per(2, 8, STATIC), per(3, 2, 8, DYNAMIC), per(2, 2, 8, DYNAMIC),
            *[per(3, n) for n in FIELDS],
            *[per(2, n) for n in FIELDS],
            per(6, 3), per(6, 3), per(2), per(6, 3), per(6, 3), per(6, 2), per(6, 2), per(6, 2), per(6, 3), per(6, 3),
            per(3, STATIC), per(3), per(3, DYNAMIC), per(3), per(3, 4, DYNAMIC),
            pltpu.SemaphoreType.DMA((2, 5)), pltpu.SemaphoreType.DMA((2,)),
            pltpu.SemaphoreType.DMA((6, 14)), pltpu.SemaphoreType.DMA((6, 14)),
        ],
        compiler_params=pltpu.CompilerParams(collective_id=0, has_side_effects=True),
    )(shift_codes, positions, velocities, thermal, offsets, occupancy)


def solution(mesh):
    in_specs = (
        P(None, None, "gx", "gy", None),
        P(None, None, "gx", "gy", None),
        P(None, None, "gx", "gy", None),
        P(None, "gx", "gy", None),
        P(None, "gx", "gy", None),
        P(),
    )
    out_specs = P(None, None, "gx", "gy", None)
    return jax.shard_map(local, mesh=mesh, in_specs=in_specs, out_specs=out_specs, check_vma=False)
```

profile of v0, /device:TPU:2, one launch (start us, length us, event | category | flops | bytes accessed | tf_op | source)
XLA Modules:
  0.0 50.4 jit_solution(6077588177074246602)
XLA Ops:
  0.0 48.0 %shard_map.64 = f32[3,12,2,16,256]{4,3,2,1,0:T(8,128)} custom-call(s32[3]{0:T(128)} %shift_ref.1, f32[3,12,2,16,256]{4,3,2,1,0:T(8,128)} %pos_h.1, f32[3,12,2,16,256]{4,3,2,1,0:T(8,128)} %vel_h.1, f32[3,12,2,16,256]{4,3,2,1,0:T(8,128)} %th_h.1, s32[12,2,16,256]{3,2,1,0:T(8,128)} %off_h.1, s32[12,2,16,256]{3,2,1,0:T(8,128)} %occ_h.1), custom_call_target="tpu_custom_call" | custom-call | tf_op jit(solution)/shard_map/pallas_call | solution.py:403
  48.0 2.4 %copy.8 = f32[3,12,2,16,256]{4,3,2,1,0:T(8,128)} copy(f32[3,12,2,16,256]{4,3,2,1,0:T(8,128)} %shard_map.64) | data formatting | bytes 2359296
where the time goes:
time: 50.7 us; the launch traced here: 50.4 us
  Pallas kernels  48 us (95%)
  local copies, waits for them, and re-layouts  2.42 us (5%)
    pallas_call x1, Pallas kernels, local(): pl.pallas_call(kernel, out_shape=jax.ShapeDtypeStruct(positions.shape, f3...  48 us
    unnamed x1, local copies, waits for them, and re-layouts  2.42 us

commit v1 on v0

--- a/solution.py
+++ b/solution.py
@@ -16,16 +16,19 @@
 ROW_PARTS = {O: ((0, 1),), M: ((0, 0), (1, 0)), I: ((1, 1),)}
 STATIC, DYNAMIC = 10, 6
 FIELDS = (STATIC, DYNAMIC) * 3
-XMSG = ("bulk", "edge", "dup", "ddown")
+A, B, C, D = 0, 1, 2, 3
+GROUP = (A, A, B, C, B, D)
+BASE = (0, STATIC, 0, 0, STATIC, 0)
+SPAN = (16, 24, 8, 8)
 
 
 def kernel(
-    shift_ref, pos_h, vel_h, th_h, off_h, occ_h, out_ref,
+    shift_h, pos_h, vel_h, th_h, off_h, occ_h, out_ref,
     pos, vel, th, off, occ, code, gs, gd, wb,
     es0, ed0, es1, ed1, es2, ed2,
     rb0, rb1, rb2, rb3, rb4, rb5,
-    sd, su, sdz, ru, rd, rxe, rxu, rxd, cm, ct, op, ope, tm, te, tr,
-    in_sem, out_sem, s_sem, r_sem,
+    sd, su, sdz, ru, rd, rxe, rxu, rxd, cy, cm, ct, op, ope, tm, te, tr,
+    shift_s, in_sem, shift_sem, s_sem, r_sem, sb_sem, rb_sem,
 ):
     es, ed = (es0, es1, es2), (ed0, ed1, ed2)
     e = (es0, ed0, es1, ed1, es2, ed2)
@@ -37,7 +40,6 @@
     on_gx = gx + 1 - 2 * core
     up, down = lax.rem(gy + 1, ngy), lax.rem(gy + ngy - 1, ngy)
     rows = (core, 1 - core)
-    sh = [shift_ref[0], shift_ref[1], shift_ref[2]]
 
     copies = []
     for r in (0, 1):
@@ -46,10 +48,19 @@
             c = pltpu.make_async_copy(view, dst.at[r], in_sem.at[r, t])
             c.start()
             copies.append(c)
+        if r == 0:
+            shift_copy = pltpu.make_async_copy(shift_h, shift_s, shift_sem)
+            shift_copy.start()
 
     barrier = pltpu.get_barrier_semaphore()
     for to in ((off_gx, gy), (on_gx, gy), (gx, up), (gx, down), (off_gx, up), (off_gx, down), (on_gx, up), (on_gx, down)):
         pl.semaphore_signal(barrier, inc=1, device_id=to, device_id_type=MESH)
+
+    sdz[...] = jnp.zeros_like(sdz)
+    su[...] = jnp.zeros_like(su)
+    te[...] = jnp.zeros_like(te)
+    shift_copy.wait()
+    sh = [shift_s[0], shift_s[1], shift_s[2]]
 
     core_f = core.astype(f32)
     xbit = {(0, 1): 1.0 - core_f, (0, 0): core_f, (1, 1): core_f, (1, 0): 1.0 - core_f}
@@ -152,8 +163,8 @@
     is_first = lax.broadcasted_iota(jnp.int32, (16, 256), 0) == 0
 
     def assemble(ph, row, source, field):
-        n = FIELDS[ph]
-        for f in range(n):
+        g, base = GROUP[ph], BASE[ph]
+        for f in range(FIELDS[ph]):
             planes = []
             for bz in (0, 1):
                 total = [None, None]
@@ -162,59 +173,105 @@
                         load = functools.partial(source, r, p * 4 + by * 2 + bz)
                         v = field(load, f, xbit[r, p], by, bz)
                         total[by] = v if total[by] is None else total[by] + v
-                sdz[bz, f : f + 1] = total[1][0:1]
+                sdz[bz, base + f : base + f + 1] = total[1][0:1]
                 planes.append(total[0] + jnp.where(not_last, pltpu.roll(total[1], 15, 0), 0.0))
             whole = planes[0] + pltpu.roll(planes[1], 255, 1)
             e[ph][row, f] = whole
-            su[ph, row, f : f + 1] = whole[15:16]
-        sd[ph, row] = sdz[0] + pltpu.roll(sdz[1], 255, 1)
-
-    def remote(ph, j, src, dst, to):
+            su[g, row, base + f : base + f + 1] = whole[15:16]
+
+    def edges(g, row):
+        n = SPAN[g]
+        sd[g, row, 0:n] = sdz[0, 0:n] + pltpu.roll(sdz[1, 0:n], 255, 1)
+
+    def remote(src, dst, send, recv, to):
         return pltpu.make_async_remote_copy(
-            src_ref=src, dst_ref=dst, send_sem=s_sem.at[ph, j], recv_sem=r_sem.at[ph, j], device_id=to, device_id_type=MESH
+            src_ref=src, dst_ref=dst, send_sem=send, recv_sem=recv, device_id=to, device_id_type=MESH
         )
 
-    def messages(ph, row):
-        n = 16 if ph == -1 else FIELDS[ph]
-        fs = pl.ds(0, 8 if n <= 8 else 16)
-        low, high = sd.at[ph, row, fs], su.at[ph, row, fs]
-        out = [
-            remote(ph, 8 + 2 * row, low, ru.at[ph, row, fs], (gx, down)),
-            remote(ph, 9 + 2 * row, high, rd.at[ph, row, fs], (gx, up)),
+    def small(g, j, src, dst, to):
+        return remote(src, dst, s_sem.at[g, j], r_sem.at[g, j], to)
+
+    def y_messages(g, row):
+        fs = pl.ds(0, SPAN[g])
+        return [
+            small(g, 6 + 2 * row, sd.at[g, row, fs], ru.at[g, row, fs], (gx, down)),
+            small(g, 7 + 2 * row, su.at[g, row, fs], rd.at[g, row, fs], (gx, up)),
         ]
-        if row != M:
-            side = 0 if row == O else 1
-            to = off_gx if row == O else on_gx
-            out += [
-                remote(ph, 4 * side + 2, low, rxu.at[ph, side, fs], (to, down)),
-                remote(ph, 4 * side + 3, high, rxd.at[ph, side, fs], (to, up)),
-                remote(ph, 4 * side + 1, low, rxe.at[ph, side, fs], (to, gy)),
-                remote(ph, 4 * side, e[ph].at[row], rb[ph].at[side], (to, gy)),
-            ]
+
+    def x_messages(g, row):
+        if row == M:
+            return []
+        fs = pl.ds(0, SPAN[g])
+        side, to = (0, off_gx) if row == O else (1, on_gx)
+        low, high = sd.at[g, row, fs], su.at[g, row, fs]
+        if g == B:
+            return [small(g, 3 * side, cy.at[side, fs], rxe.at[g, side, fs], (to, gy))]
+        return [
+            small(g, 3 * side + 1, low, rxu.at[g, side, fs], (to, down)),
+            small(g, 3 * side + 2, high, rxd.at[g, side, fs], (to, up)),
+            small(g, 3 * side, low, rxe.at[g, side, fs], (to, gy)),
+        ]
+
+    def bulk(ph, row, halves=(0, 1)):
+        side, to = (0, off_gx) if row == O else (1, on_gx)
+        if row == M:
+            return []
+        if GROUP[ph] != B:
+            return [remote(e[ph].at[row], rb[ph].at[side], sb_sem.at[ph, side, 0], rb_sem.at[ph, side, 0], (to, gy))]
+        out = []
+        for h in halves:
+            cols = pl.ds(8 * h, 8)
+            src, dst = e[ph].at[row, :, cols], rb[ph].at[side, :, cols]
+            out.append(remote(src, dst, sb_sem.at[ph, side, h], rb_sem.at[ph, side, h], (to, gy)))
         return out
 
-    def send(ph, row):
-        for c in messages(ph, row):
+    def start(messages):
+        for c in messages:
             c.start()
 
-    def receive(ph, row):
-        for c in messages(ph, row):
+    def arrive(messages):
+        for c in messages:
             c.wait_recv()
 
-    def totals(ph, row):
-        low, high = sd[ph, row] + rd[ph, row], ru[ph, row]
-        if row != M:
-            side = 0 if row == O else 1
-            low = low + rxe[ph, side] + rxd[ph, side]
-            high = high + rxu[ph, side]
-        cm[ph, row] = low
-        ct[ph, row] = high
+    def combine(row):
+        side = 0 if row == O else 1
+        arrive(y_messages(B, row))
+        cy[side] = sd[B, row] + rd[B, row]
+        for ph in (2, 4):
+            for f in range(STATIC):
+                k = BASE[ph] + f
+                e[ph][row, f, 8:16] = e[ph][row, f, 8:16] + jnp.where(is_last[8:16], ru[B, row, k : k + 1], 0.0)
+        start(x_messages(B, row))
+
+    def totals(g, row):
+        n = SPAN[g]
+        side = 0 if row == O else 1
+        if g != B or row == M:
+            arrive(y_messages(g, row))
+        arrive(x_messages(g, row))
+        if row == M:
+            low, high = sd[g, row, 0:n] + rd[g, row, 0:n], ru[g, row, 0:n]
+        elif g == B:
+            low, high = cy[side] + rxe[g, side], None
+        else:
+            low = sd[g, row, 0:n] + rd[g, row, 0:n] + rxe[g, side, 0:n] + rxd[g, side, 0:n]
+            high = ru[g, row, 0:n] + rxu[g, side, 0:n]
+        cm[g, row, 0:n] = low
+        if high is not None:
+            ct[g, row, 0:n] = high
+
+    def rim(ph, row, f):
+        k = BASE[ph] + f
+        return cm[GROUP[ph], row, k : k + 1]
 
     def total(ph, row, f):
         v = e[ph][row, f]
         if row != M:
             v = v + rb[ph][0 if row == O else 1, f]
-        return v + jnp.where(is_last, ct[ph, row, f : f + 1], 0.0)
+            if GROUP[ph] == B:
+                return v
+        k = BASE[ph] + f
+        return v + jnp.where(is_last, ct[GROUP[ph], row, k : k + 1], 0.0)
 
     def invert(a):
         n, sx, sy, sz, xx, yy, zz, xy, xz, yz = a
@@ -244,14 +301,14 @@
     def static_solve(s, row):
         for f, v in enumerate(invert([total(2 * s, row, f) for f in range(STATIC)])):
             op[row, f] = v
-        o = invert([cm[2 * s, row, f : f + 1] for f in range(STATIC)])
+        o = invert([rim(2 * s, row, f) for f in range(STATIC)])
         for f, v in enumerate(o):
             ope[row, f : f + 1] = v
 
     def dynamic_solve(s, row):
         ph = 2 * s + 1
         t = respond([op[row, f] for f in range(STATIC)], [total(ph, row, f) for f in range(DYNAMIC)])
-        x = respond([ope[row, f : f + 1] for f in range(STATIC)], [cm[ph, row, f : f + 1] for f in range(DYNAMIC)])
+        x = respond([ope[row, f : f + 1] for f in range(STATIC)], [rim(ph, row, f) for f in range(DYNAMIC)])
         for f in range(DYNAMIC):
             te[row, f : f + 1] = x[f]
             tm[row, f] = t[f]
@@ -271,9 +328,9 @@
             ax, az = ax - oz, az + ox
         return [ax, ay + bx * oz, az - bx * oy, ox, oy, oz]
 
-    def advance(s, r):
+    def advance(s, r, parts):
         delta = sh[0] ^ sh[s - 1]
-        for p in (0, 1):
+        for p in parts:
             row = M if p == 0 else (O if r == 0 else I)
             for q in range(4):
                 g = p * 4 + q
@@ -301,109 +358,141 @@
         delta = sh[s - 1] ^ sh[s]
         return lambda r, g, f: wb[s - 1, r, g ^ delta, f]
 
-    def finish(r):
+    def finish(r, parts):
         delta = sh[0] ^ sh[2]
         def body(ys, zs):
-            tables = []
-            for p in (0, 1):
+            tables = {}
+            for p in parts:
                 row = M if p == 0 else (O if r == 0 else I)
                 for q in range(4):
                     t = [tr[row, q, f, ys, zs] for f in range(6)]
-                    tables.append(offset(t, xbit[r, p], q // 2, q % 2))
+                    tables[p, q] = offset(t, xbit[r, p], q // 2, q % 2)
             for m in range(SLOTS):
                 k = code[r, m, ys, zs] ^ delta
                 bz, by, bx = (k & 1) == 1, (k & 2) == 2, (k & 4) == 4
                 t = []
                 for f in range(6):
-                    c = [jnp.where(bz, tables[2 * j + 1][f], tables[2 * j][f]) for j in range(4)]
-                    c = [jnp.where(by, c[1], c[0]), jnp.where(by, c[3], c[2])]
-                    t.append(jnp.where(bx, c[1], c[0]))
+                    c = []
+                    for p in parts:
+                        low = jnp.where(bz, tables[p, 1][f], tables[p, 0][f])
+                        c.append(jnp.where(by, jnp.where(bz, tables[p, 3][f], tables[p, 2][f]), low))
+                    t.append(c[0] if len(c) == 1 else jnp.where(bx, c[1], c[0]))
                 ax, ay, az, ox, oy, oz = t
                 x, y, z = (pos[r, a, m, ys, zs] for a in range(3))
                 hot = [th[r, a, (m + 2) % SLOTS, ys, zs] for a in range(3)]
-                live = k < 8
-                out_ref[0, m, rows[r], ys, zs] = jnp.where(live, hot[0] + ax + (oy * z - oz * y), 0.0)
-                out_ref[1, m, rows[r], ys, zs] = jnp.where(live, hot[1] + ay + (oz * x - ox * z), 0.0)
-                out_ref[2, m, rows[r], ys, zs] = jnp.where(live, hot[2] + az + (ox * y - oy * x), 0.0)
+                fresh = [hot[0] + ax + (oy * z - oz * y), hot[1] + ay + (oz * x - ox * z), hot[2] + az + (ox * y - oy * x)]
+                mine = k < 8 if parts != (1,) else (k & 12) == 4
+                for a in range(3):
+                    rest = out_ref[a, m, rows[r], ys, zs] if parts == (1,) else 0.0
+                    out_ref[a, m, rows[r], ys, zs] = jnp.where(mine, fresh[a], rest)
         chunked(body)
 
-    sdz[...] = jnp.zeros_like(sdz)
-    su[...] = jnp.zeros_like(su)
-    te[...] = jnp.zeros_like(te)
-    for t in range(5):
+    for t in (0, 1, 2):
         copies[t].wait()
     make_codes(0)
     static_moments(0, 1)
+    assemble(0, O, static_source(0), static_field)
+    pl.semaphore_wait(barrier, 8)
+    start(bulk(0, O))
+    for t in (3, 4):
+        copies[t].wait()
     dynamic_moments(0, 0, 1)
-    assemble(0, O, static_source(0), static_field)
     assemble(1, O, dynamic_source(0), dynamic_field)
-    pl.semaphore_wait(barrier, 8)
-    send(0, O)
-    send(1, O)
+    edges(A, O)
+    start(y_messages(A, O) + x_messages(A, O))
     static_moments(0, 0)
     assemble(2, O, static_source(1), static_field)
-    send(2, O)
-    dynamic_moments(0, 0, 0)
+    assemble(4, O, static_source(2), static_field)
+    edges(B, O)
+    start(y_messages(B, O) + bulk(1, O))
     for t in range(5, 10):
         copies[t].wait()
     make_codes(1)
-    for p in (0, 1):
-        static_moments(1, p)
-        dynamic_moments(0, 1, p)
-    for row in (M, I):
-        assemble(0, row, static_source(0), static_field)
-        assemble(1, row, dynamic_source(0), dynamic_field)
-        send(0, row)
-        send(1, row)
-    for row in (M, I):
+    static_moments(1, 1)
+    dynamic_moments(0, 1, 1)
+    assemble(0, I, static_source(0), static_field)
+    assemble(1, I, dynamic_source(0), dynamic_field)
+    edges(A, I)
+    start(y_messages(A, I) + x_messages(A, I) + bulk(0, I) + bulk(1, I))
+    dynamic_moments(0, 0, 0)
+    static_moments(1, 0)
+    dynamic_moments(0, 1, 0)
+    assemble(0, M, static_source(0), static_field)
+    assemble(1, M, dynamic_source(0), dynamic_field)
+    edges(A, M)
+    start(y_messages(A, M) + bulk(2, O, (0,)))
+    for row in (I, M):
         assemble(2, row, static_source(1), static_field)
-        send(2, row)
-    for row in (M, I, O):
         assemble(4, row, static_source(2), static_field)
-        if row != O:
-            send(4, row)
-    for r in (0, 1):
-        for p in (0, 1):
-            dynamic_moments(1, r, p)
+        edges(B, row)
+        start(y_messages(B, row))
+    combine(O)
+    start(bulk(2, O, (1,)))
+    dynamic_moments(1, 0, 0)
+    dynamic_moments(1, 0, 1)
+    dynamic_moments(1, 1, 0)
+    dynamic_moments(1, 1, 1)
     for s in (0, 1, 2):
-        for row in (M, I, O):
-            receive(2 * s, row)
-            totals(2 * s, row)
+        for row in (M, I):
+            if s < 2:
+                totals((A, B)[s], row)
+            arrive(bulk(2 * s, row))
             static_solve(s, row)
-        for row in (M, I, O):
-            receive(2 * s + 1, row)
-            totals(2 * s + 1, row)
+            if s > 0:
+                totals((C, D)[s - 1], row)
+            arrive(bulk(2 * s + 1, row))
             dynamic_solve(s, row)
         if s < 2:
-            advance(s + 1, 0)
-            assemble(2 * s + 3, O, dynamic_source(s + 1), dynamic_field)
-            send(2 * s + 3, O)
+            advance(s + 1, 1, (0, 1))
+            assemble(2 * s + 3, I, dynamic_source(s + 1), dynamic_field)
+            edges((C, D)[s], I)
+            start(y_messages((C, D)[s], I) + x_messages((C, D)[s], I) + bulk(2 * s + 3, I))
+            advance(s + 1, 0, (0,))
+        else:
+            finish(1, (0, 1))
+            finish(0, (0,))
+        if s < 2:
+            totals((A, B)[s], O)
+        arrive(bulk(2 * s, O))
+        static_solve(s, O)
+        if s > 0:
+            totals((C, D)[s - 1], O)
+        arrive(bulk(2 * s + 1, O))
+        dynamic_solve(s, O)
+        if s < 2:
+            advance(s + 1, 0, (1,))
+            for row in (O, M):
+                assemble(2 * s + 3, row, dynamic_source(s + 1), dynamic_field)
+                edges((C, D)[s], row)
+                start(y_messages((C, D)[s], row) + x_messages((C, D)[s], row))
+            start(bulk(2 * s + 3, O))
             if s == 0:
-                send(4, O)
-            advance(s + 1, 1)
-            for row in (M, I):
-                assemble(2 * s + 3, row, dynamic_source(s + 1), dynamic_field)
-                send(2 * s + 3, row)
-            if s == 0:
-                for r in (0, 1):
-                    for p in (0, 1):
-                        dynamic_moments(2, r, p)
-    for r in (0, 1):
-        finish(r)
-    for ph in range(6):
-        for row in (O, M, I):
-            for c in messages(ph, row):
+                start(bulk(4, O))
+                dynamic_moments(2, 0, 0)
+                dynamic_moments(2, 0, 1)
+                combine(I)
+                start(bulk(2, I) + bulk(4, I))
+                dynamic_moments(2, 1, 0)
+                dynamic_moments(2, 1, 1)
+        else:
+            finish(0, (1,))
+    for row in (O, M, I):
+        for g in range(4):
+            for c in y_messages(g, row) + x_messages(g, row):
                 c.wait_send()
+        for ph in range(6):
+            for c in bulk(ph, row):
+                c.wait_send()
 
 
 def local(positions, velocities, thermal, offsets, occupancy, shift_codes):
-    any_space = pl.BlockSpec(memory_space=pl.ANY)
-    rows = lambda n: pltpu.VMEM((n, 16, 256), f32)
+    any_space = pl.BlockSpec(memory_space=pltpu.HBM)
+    rim = lambda *lead: pltpu.VMEM((*lead, 24, 256), f32)
     per = lambda *lead: pltpu.VMEM((*lead, 16, 256), f32)
     return pl.pallas_call(
         kernel,
         out_shape=jax.ShapeDtypeStruct(positions.shape, f32),
-        in_specs=[pl.BlockSpec(memory_space=pltpu.SMEM)] + [any_space] * 5,
+        in_specs=[any_space] * 6,
         out_specs=pl.BlockSpec(memory_space=pltpu.VMEM),
         scratch_shapes=[
             per(2, 3, SLOTS), per(2, 3, SLOTS), per(2, 3, SLOTS),
@@ -411,13 +500,16 @@
             per(2, 8, STATIC), per(3, 2, 8, DYNAMIC), per(2, 2, 8, DYNAMIC),
             *[per(3, n) for n in FIELDS],
             *[per(2, n) for n in FIELDS],
-            per(6, 3), per(6, 3), per(2), per(6, 3), per(6, 3), per(6, 2), per(6, 2), per(6, 2), per(6, 3), per(6, 3),
+            rim(4, 3), rim(4, 3), rim(2), rim(4, 3), rim(4, 3), rim(4, 2), rim(4, 2), rim(4, 2), rim(2), rim(4, 3), rim(4, 3),
             per(3, STATIC), per(3), per(3, DYNAMIC), per(3), per(3, 4, DYNAMIC),
-            pltpu.SemaphoreType.DMA((2, 5)), pltpu.SemaphoreType.DMA((2,)),
-            pltpu.SemaphoreType.DMA((6, 14)), pltpu.SemaphoreType.DMA((6, 14)),
+            pltpu.SMEM((3,), jnp.int32), pltpu.SemaphoreType.DMA((2, 5)), pltpu.SemaphoreType.DMA,
+            pltpu.SemaphoreType.DMA((4, 12)), pltpu.SemaphoreType.DMA((4, 12)),
+            pltpu.SemaphoreType.DMA((6, 2, 2)), pltpu.SemaphoreType.DMA((6, 2, 2)),
         ],
-        compiler_params=pltpu.CompilerParams(collective_id=0, has_side_effects=True),
-    )(shift_codes, positions, velocities, thermal, offsets, occupancy)
+        compiler_params=pltpu.CompilerParams(
+            collective_id=0, has_side_effects=True, vmem_limit_bytes=40 * 1024 * 1024
+        ),
+    )(*(pltpu.with_memory_space_constraint(v, pltpu.HBM) for v in (shift_codes, positions, velocities, thermal, offsets, occupancy)))
 
 
 def solution(mesh):

time: 50.7 us -> 39.1 us (0.77)
  Pallas kernels: 48 us -> 38 us
  local copies, waits for them, and re-layouts: 2.42 us -> 1.02 us
    pallas_call x1, Pallas kernels: 48 us -> 38 us  [local(): pl.pallas_call(kernel, out_shape=jax.ShapeDtypeStruct(positions.shape, f3...]
    unnamed x1, local copies, waits for them, and re-layouts: 2.42 us -> 1.02 us
where the time goes in v1:
time: 39.1 us; the launch traced here: 39 us
  Pallas kernels  38 us (97%)
  local copies, waits for them, and re-layouts  1.02 us (3%)
    pallas_call x1, Pallas kernels, local(): pl.pallas_call(kernel, out_shape=jax.ShapeDtypeStruct(positions.shape, f3...  38 us
    unnamed x1, local copies, waits for them, and re-layouts  1.02 us

profile of v1, /device:TPU:2, one launch (start us, length us, event | category | flops | bytes accessed | tf_op | source)
XLA Modules:
  0.0 39.0 jit_solution(7233569049747099386)
XLA Ops:
  0.0 38.0 %shard_map.64 = f32[3,12,2,16,256]{4,3,2,1,0:T(8,128)S(1)} custom-call(s32[3]{0:T(128)} %shift_h.1, f32[3,12,2,16,256]{4,3,2,1,0:T(8,128)} %pos_h.1, f32[3,12,2,16,256]{4,3,2,1,0:T(8,128)} %vel_h.1, f32[3,12,2,16,256]{4,3,2,1,0:T(8,128)} %th_h.1, s32[12,2,16,256]{3,2,1,0:T(8,128)} %off_h.1, s32[12,2,16,256]{3,2,1,0:T(8,128)} %occ_h.1), custom_call_target="tpu_custom_call" | custom-call | tf_op jit(solution)/shard_map/pallas_call | solution.py:492
  38.0 1.0 %copy.8 = f32[3,12,2,16,256]{4,3,2,1,0:T(8,128)} copy(f32[3,12,2,16,256]{4,3,2,1,0:T(8,128)S(1)} %shard_map.64) | data formatting | bytes 2359296

commit v2 on v1

--- a/solution.py
+++ b/solution.py
@@ -16,10 +16,10 @@
 ROW_PARTS = {O: ((0, 1),), M: ((0, 0), (1, 0)), I: ((1, 1),)}
 STATIC, DYNAMIC = 10, 6
 FIELDS = (STATIC, DYNAMIC) * 3
-A, B, C, D = 0, 1, 2, 3
-GROUP = (A, A, B, C, B, D)
-BASE = (0, STATIC, 0, 0, STATIC, 0)
-SPAN = (16, 24, 8, 8)
+A, B, C, E, D = 0, 1, 2, 3, 4
+GROUP = (A, A, B, C, E, D)
+BASE = (0, STATIC, 0, 0, 0, 0)
+SPAN = (16, 16, 8, 16, 8)
 
 
 def kernel(
@@ -27,8 +27,8 @@
     pos, vel, th, off, occ, code, gs, gd, wb,
     es0, ed0, es1, ed1, es2, ed2,
     rb0, rb1, rb2, rb3, rb4, rb5,
-    sd, su, sdz, ru, rd, rxe, rxu, rxd, cy, cm, ct, op, ope, tm, te, tr,
-    shift_s, in_sem, shift_sem, s_sem, r_sem, sb_sem, rb_sem,
+    sd, su, sdz, ry, rx, everything, cy, cm, ct, op, ope, tm, te, tr,
+    shift_s, in_sem, shift_sem, s_sem, r_sem, rb_sem,
 ):
     es, ed = (es0, es1, es2), (ed0, ed1, ed2)
     e = (es0, ed0, es1, ed1, es2, ed2)
@@ -189,13 +189,13 @@
         )
 
     def small(g, j, src, dst, to):
-        return remote(src, dst, s_sem.at[g, j], r_sem.at[g, j], to)
+        return remote(src, dst, s_sem, r_sem.at[g, j], to)
 
     def y_messages(g, row):
         fs = pl.ds(0, SPAN[g])
         return [
-            small(g, 6 + 2 * row, sd.at[g, row, fs], ru.at[g, row, fs], (gx, down)),
-            small(g, 7 + 2 * row, su.at[g, row, fs], rd.at[g, row, fs], (gx, up)),
+            small(g, row, sd.at[g, row, fs], ry.at[g, row, 0, fs], (gx, down)),
+            small(g, row, su.at[g, row, fs], ry.at[g, row, 1, fs], (gx, up)),
         ]
 
     def x_messages(g, row):
@@ -205,11 +205,11 @@
         side, to = (0, off_gx) if row == O else (1, on_gx)
         low, high = sd.at[g, row, fs], su.at[g, row, fs]
         if g == B:
-            return [small(g, 3 * side, cy.at[side, fs], rxe.at[g, side, fs], (to, gy))]
+            return [small(g, 3 + side, cy.at[side, fs], rx.at[g, side, 0, fs], (to, gy))]
         return [
-            small(g, 3 * side + 1, low, rxu.at[g, side, fs], (to, down)),
-            small(g, 3 * side + 2, high, rxd.at[g, side, fs], (to, up)),
-            small(g, 3 * side, low, rxe.at[g, side, fs], (to, gy)),
+            small(g, 3 + side, low, rx.at[g, side, 1, fs], (to, down)),
+            small(g, 3 + side, high, rx.at[g, side, 2, fs], (to, up)),
+            small(g, 3 + side, low, rx.at[g, side, 0, fs], (to, gy)),
         ]
 
     def bulk(ph, row, halves=(0, 1)):
@@ -217,45 +217,55 @@
         if row == M:
             return []
         if GROUP[ph] != B:
-            return [remote(e[ph].at[row], rb[ph].at[side], sb_sem.at[ph, side, 0], rb_sem.at[ph, side, 0], (to, gy))]
+            return [remote(e[ph].at[row], rb[ph].at[side], s_sem, rb_sem.at[ph, side], (to, gy))]
         out = []
         for h in halves:
             cols = pl.ds(8 * h, 8)
             src, dst = e[ph].at[row, :, cols], rb[ph].at[side, :, cols]
-            out.append(remote(src, dst, sb_sem.at[ph, side, h], rb_sem.at[ph, side, h], (to, gy)))
+            out.append(remote(src, dst, s_sem, rb_sem.at[ph, side], (to, gy)))
         return out
 
     def start(messages):
         for c in messages:
             c.start()
 
-    def arrive(messages):
-        for c in messages:
-            c.wait_recv()
+    def arrive_y(g, row):
+        view = ry.at[g, row, :, pl.ds(0, SPAN[g])]
+        remote(view, view, s_sem, r_sem.at[g, row], (gx, up)).wait_recv()
+
+    def arrive_x(g, row):
+        side = 0 if row == O else 1
+        if row != M:
+            view = rx.at[g, side, pl.ds(0, 1 if g == B else 3), pl.ds(0, SPAN[g])]
+            remote(view, view, s_sem, r_sem.at[g, 3 + side], (gx, up)).wait_recv()
+
+    def arrive_bulk(ph, row):
+        side = 0 if row == O else 1
+        if row != M:
+            view = rb[ph].at[side]
+            remote(view, view, s_sem, rb_sem.at[ph, side], (gx, up)).wait_recv()
 
     def combine(row):
         side = 0 if row == O else 1
-        arrive(y_messages(B, row))
-        cy[side] = sd[B, row] + rd[B, row]
-        for ph in (2, 4):
-            for f in range(STATIC):
-                k = BASE[ph] + f
-                e[ph][row, f, 8:16] = e[ph][row, f, 8:16] + jnp.where(is_last[8:16], ru[B, row, k : k + 1], 0.0)
+        arrive_y(B, row)
+        cy[side] = sd[B, row] + ry[B, row, 1]
+        for f in range(STATIC):
+            e[2][row, f, 8:16] = e[2][row, f, 8:16] + jnp.where(is_last[8:16], ry[B, row, 0, f : f + 1], 0.0)
         start(x_messages(B, row))
 
     def totals(g, row):
         n = SPAN[g]
         side = 0 if row == O else 1
         if g != B or row == M:
-            arrive(y_messages(g, row))
-        arrive(x_messages(g, row))
+            arrive_y(g, row)
+        arrive_x(g, row)
         if row == M:
-            low, high = sd[g, row, 0:n] + rd[g, row, 0:n], ru[g, row, 0:n]
+            low, high = sd[g, row, 0:n] + ry[g, row, 1, 0:n], ry[g, row, 0, 0:n]
         elif g == B:
-            low, high = cy[side] + rxe[g, side], None
+            low, high = cy[side] + rx[g, side, 0], None
         else:
-            low = sd[g, row, 0:n] + rd[g, row, 0:n] + rxe[g, side, 0:n] + rxd[g, side, 0:n]
-            high = ru[g, row, 0:n] + rxu[g, side, 0:n]
+            low = sd[g, row, 0:n] + ry[g, row, 1, 0:n] + rx[g, side, 0, 0:n] + rx[g, side, 2, 0:n]
+            high = ry[g, row, 0, 0:n] + rx[g, side, 1, 0:n]
         cm[g, row, 0:n] = low
         if high is not None:
             ct[g, row, 0:n] = high
@@ -402,7 +412,6 @@
     start(y_messages(A, O) + x_messages(A, O))
     static_moments(0, 0)
     assemble(2, O, static_source(1), static_field)
-    assemble(4, O, static_source(2), static_field)
     edges(B, O)
     start(y_messages(B, O) + bulk(1, O))
     for t in range(5, 10):
@@ -423,24 +432,25 @@
     start(y_messages(A, M) + bulk(2, O, (0,)))
     for row in (I, M):
         assemble(2, row, static_source(1), static_field)
-        assemble(4, row, static_source(2), static_field)
         edges(B, row)
         start(y_messages(B, row))
     combine(O)
     start(bulk(2, O, (1,)))
+    for row in (O, M, I):
+        assemble(4, row, static_source(2), static_field)
+        edges(E, row)
     dynamic_moments(1, 0, 0)
     dynamic_moments(1, 0, 1)
     dynamic_moments(1, 1, 0)
     dynamic_moments(1, 1, 1)
     for s in (0, 1, 2):
         for row in (M, I):
-            if s < 2:
-                totals((A, B)[s], row)
-            arrive(bulk(2 * s, row))
+            totals((A, B, E)[s], row)
+            arrive_bulk(2 * s, row)
             static_solve(s, row)
             if s > 0:
                 totals((C, D)[s - 1], row)
-            arrive(bulk(2 * s + 1, row))
+            arrive_bulk(2 * s + 1, row)
             dynamic_solve(s, row)
         if s < 2:
             advance(s + 1, 1, (0, 1))
@@ -451,13 +461,12 @@
         else:
             finish(1, (0, 1))
             finish(0, (0,))
-        if s < 2:
-            totals((A, B)[s], O)
-        arrive(bulk(2 * s, O))
+        totals((A, B, E)[s], O)
+        arrive_bulk(2 * s, O)
         static_solve(s, O)
         if s > 0:
             totals((C, D)[s - 1], O)
-        arrive(bulk(2 * s + 1, O))
+        arrive_bulk(2 * s + 1, O)
         dynamic_solve(s, O)
         if s < 2:
             advance(s + 1, 0, (1,))
@@ -467,28 +476,24 @@
                 start(y_messages((C, D)[s], row) + x_messages((C, D)[s], row))
             start(bulk(2 * s + 3, O))
             if s == 0:
-                start(bulk(4, O))
                 dynamic_moments(2, 0, 0)
                 dynamic_moments(2, 0, 1)
                 combine(I)
-                start(bulk(2, I) + bulk(4, I))
+                start(bulk(2, I))
+                start(y_messages(E, I) + x_messages(E, I) + bulk(4, I))
                 dynamic_moments(2, 1, 0)
                 dynamic_moments(2, 1, 1)
+                for row in (M, O):
+                    start(y_messages(E, row) + x_messages(E, row))
+                start(bulk(4, O))
         else:
             finish(0, (1,))
-    for row in (O, M, I):
-        for g in range(4):
-            for c in y_messages(g, row) + x_messages(g, row):
-                c.wait_send()
-        for ph in range(6):
-            for c in bulk(ph, row):
-                c.wait_send()
+    remote(everything, everything, s_sem, r_sem.at[0, 0], (gx, up)).wait_send()
 
 
 def local(positions, velocities, thermal, offsets, occupancy, shift_codes):
     any_space = pl.BlockSpec(memory_space=pltpu.HBM)
-    rim = lambda *lead: pltpu.VMEM((*lead, 24, 256), f32)
-    per = lambda *lead: pltpu.VMEM((*lead, 16, 256), f32)
+    per = rim = lambda *lead: pltpu.VMEM((*lead, 16, 256), f32)
     return pl.pallas_call(
         kernel,
         out_shape=jax.ShapeDtypeStruct(positions.shape, f32),
@@ -500,11 +505,10 @@
             per(2, 8, STATIC), per(3, 2, 8, DYNAMIC), per(2, 2, 8, DYNAMIC),
             *[per(3, n) for n in FIELDS],
             *[per(2, n) for n in FIELDS],
-            rim(4, 3), rim(4, 3), rim(2), rim(4, 3), rim(4, 3), rim(4, 2), rim(4, 2), rim(4, 2), rim(2), rim(4, 3), rim(4, 3),
+            rim(5, 3), rim(5, 3), rim(2), rim(5, 3, 2), rim(5, 2, 3), rim(140), rim(2), rim(5, 3), rim(5, 3),
             per(3, STATIC), per(3), per(3, DYNAMIC), per(3), per(3, 4, DYNAMIC),
             pltpu.SMEM((3,), jnp.int32), pltpu.SemaphoreType.DMA((2, 5)), pltpu.SemaphoreType.DMA,
-            pltpu.SemaphoreType.DMA((4, 12)), pltpu.SemaphoreType.DMA((4, 12)),
-            pltpu.SemaphoreType.DMA((6, 2, 2)), pltpu.SemaphoreType.DMA((6, 2, 2)),
+            pltpu.SemaphoreType.DMA, pltpu.SemaphoreType.DMA((5, 5)), pltpu.SemaphoreType.DMA((6, 2)),
         ],
         compiler_params=pltpu.CompilerParams(
             collective_id=0, has_side_effects=True, vmem_limit_bytes=40 * 1024 * 1024

time: 39.1 us -> 37.9 us (0.969)
  the two profiles are of different devices: /device:TPU:2 before, /device:TPU:65 now
where the time goes in v2:
time: 37.9 us; the launch traced here: 37.8 us
  Pallas kernels  36.8 us (97%)
  local copies, waits for them, and re-layouts  1.02 us (3%)
    pallas_call x1, Pallas kernels, local(): pl.pallas_call(kernel, out_shape=jax.ShapeDtypeStruct(positions.shape, f3...  36.8 us
    unnamed x1, local copies, waits for them, and re-layouts  1.02 us

profile of v2, /device:TPU:65, one launch (start us, length us, event | category | flops | bytes accessed | tf_op | source)
XLA Modules:
  0.0 37.8 jit_solution(3369009836184267868)
XLA Ops:
  0.0 36.8 %shard_map.64 = f32[3,12,2,16,256]{4,3,2,1,0:T(8,128)S(1)} custom-call(s32[3]{0:T(128)} %shift_h.1, f32[3,12,2,16,256]{4,3,2,1,0:T(8,128)} %pos_h.1, f32[3,12,2,16,256]{4,3,2,1,0:T(8,128)} %vel_h.1, f32[3,12,2,16,256]{4,3,2,1,0:T(8,128)} %th_h.1, s32[12,2,16,256]{3,2,1,0:T(8,128)} %off_h.1, s32[12,2,16,256]{3,2,1,0:T(8,128)} %occ_h.1), custom_call_target="tpu_custom_call" | custom-call | tf_op jit(solution)/shard_map/pallas_call | solution.py:497
  36.8 1.0 %copy.8 = f32[3,12,2,16,256]{4,3,2,1,0:T(8,128)} copy(f32[3,12,2,16,256]{4,3,2,1,0:T(8,128)S(1)} %shard_map.64) | data formatting | bytes 2359296
